TPU v7x, 256 devices: a whole 4x4x8 slice. The times are simulated.
256 devices in a mesh: root: 8 (over z), virt: 16 (over x, y), occ: 2 (over core).
Axes of the slice: x: 4, y: 4, z: 8, core: 2. Of those that a mesh axis runs over, the one named last changes fastest.
Arguments:
- trial_singles: bfloat16 [16, 96], P('root'), may hold values from -6 to 6
- trial_doubles: bfloat16 [16, 480, 9216], P('root', 'virt', 'occ'), may hold values from -6 to 6
- occ_fock: bfloat16 [96, 96], replicated, may hold values from -0.625 to 0.625
- virt_fock: bfloat16 [480, 480], replicated, may hold values from -0.25 to 0.25
- w_ovoo: bfloat16 [96, 480, 9216], P('occ', 'virt', 'root'), may hold values from -0.625 to 0.625
- w_ooov: bfloat16 [96, 480, 9216], P('occ', 'virt', 'root'), may hold values from -0.0029296875 to 0.0029296875
- converged: int32 [16], replicated, may hold values from 0 to 1, as said below
Outputs:
- sigma_doubles: bfloat16 [16, 480, 9216], P('root', 'virt', 'occ')
- sigma_singles: float32 [16, 96], P('root')
- subspace: float32 [16, 16], P('root')
Inputs may be any that keep to these rules, and one draw needn't show every extreme that they name: `converged`: exactly 8 roots are active (0). In every draw at least one aligned block of 2 roots has all its roots active; other blocks may have none.
All inputs are finite; a program needn't handle non-finite values.
Results may differ from a plain program's by a relative error of at most 0.0044.
Values may be sent and summed in bfloat16 or wider, within the bound.
No kernel may reach another device: no remote copies, remote signals or barrier semaphores. Data moves between devices by JAX's collectives and lax.ppermute only.
A program may use at most 256 MiB of HBM per device.

v0:
```python
import functools
import math
import jax
import jax.numpy as jnp
from jax import lax
from jax.sharding import Mesh
from jax.sharding import PartitionSpec as P

ROOT_VIRT_OCC = ("root", "virt_0", "virt_1", "occ")
VIRT = ("virt_0", "virt_1")


def laid_out(parts, dim):
    parts = jnp.moveaxis(parts, 0, dim)
    shape = parts.shape
    return parts.reshape(*shape[:dim], shape[dim] * shape[dim + 1], *shape[dim + 2 :])


def from_everyone(array, axis):
    copies = jnp.broadcast_to(array, (lax.axis_size(axis), *array.shape))
    return lax.all_to_all(copies, axis, split_axis=0, concat_axis=0, tiled=True)


def gather_directly(array, axis, dim):
    return laid_out(from_everyone(array, axis), dim)


def by_axis(array, axes):
    return functools.reduce(lax.psum, axes, array)


def in_blocks(array, dim, devices):
    before, after = (array.shape[:dim], array.shape[dim + 1 :])
    return jnp.moveaxis(array.reshape(*before, devices, -1, *after), dim, 0)


def sum_at_owner(array, axis, dim):
    parts = in_blocks(array, dim, lax.axis_size(axis))
    arrived = lax.all_to_all(parts, axis, split_axis=0, concat_axis=0, tiled=True)
    return arrived.astype(jnp.float32).sum(axis=0)


def in_one_piece(arrays, axis, split_dim, concat_dim, along):
    ends, at = ([], 0)
    for a in arrays[:-1]:
        at += a.shape[along]
        ends.append(at)
    both = jnp.concatenate(arrays, axis=along)
    return tuple(
        jnp.split(
            lax.all_to_all(both, axis, split_axis=split_dim, concat_axis=concat_dim, tiled=True),
            ends,
            axis=along,
        )
    )


def flat_pairs(left, right):
    return lax.dot_general(
        left.reshape(left.shape[0], -1),
        right.reshape(right.shape[0], -1),
        (((1,), (1,)), ((), ())),
        preferred_element_type=jnp.float32,
    )


def local(trial_singles, trial_doubles, occ_fock, virt_fock, w_ovoo, w_ooov, converged):
    local_roots, virt_local, pair_local = trial_doubles.shape
    occ_count = occ_fock.shape[0]
    virt_count = virt_fock.shape[0]
    root_count = converged.shape[0]
    root_groups = lax.axis_size("root")
    occ_groups = lax.axis_size("occ")
    root_index = lax.axis_index("root")
    occ_index = lax.axis_index("occ")
    occ_half = occ_count // occ_groups
    block_pairs = occ_count * occ_count // root_groups
    own_start = occ_index * occ_half
    active = (1 - converged).astype(jnp.float32)
    own_active = lax.dynamic_slice_in_dim(active, root_index * local_roots, local_roots)
    singles_all = gather_directly(trial_singles, "root", 0)
    gathered = gather_directly(trial_doubles, "occ", 2)
    fock_cols = lax.dynamic_slice_in_dim(occ_fock, own_start, occ_half, 1)
    batch_rows = local_roots * virt_local
    stacked = gathered.reshape(batch_rows, occ_count, occ_count)
    first_term = jnp.einsum(
        "ki,bkj->bij", fock_cols, stacked, preferred_element_type=jnp.float32
    ).reshape(local_roots, virt_local, pair_local)
    own_rows = trial_doubles.reshape(batch_rows, occ_half, occ_count)
    second_term = jnp.einsum(
        "bik,kj->bij", own_rows, occ_fock, preferred_element_type=jnp.float32
    ).reshape(local_roots, virt_local, pair_local)
    doubles_block = lax.all_to_all(gathered, "root", split_axis=2, concat_axis=0, tiled=True)
    partial_coupling = flat_pairs(doubles_block, w_ooov)
    coupling_part = lax.dynamic_update_slice(
        jnp.zeros((root_count, occ_count), jnp.float32), partial_coupling, (jnp.int32(0), own_start)
    )
    coupling = by_axis(coupling_part, ROOT_VIRT_OCC)
    singles_fock = jnp.dot(singles_all, occ_fock, preferred_element_type=jnp.float32)
    singles_every = active[:, None] * (-singles_fock - 0.5 * coupling)
    sigma_singles = lax.dynamic_slice_in_dim(singles_every, root_index * local_roots, local_roots)
    singles_cols = lax.dynamic_slice_in_dim(singles_all, own_start, occ_half, 1)
    outer_part = (
        -jnp.dot(singles_cols, w_ovoo.reshape(occ_half, -1), preferred_element_type=jnp.float32)
    ).reshape(root_count, virt_local, block_pairs)
    product = jnp.einsum(
        "ac,ncp->nap",
        virt_fock,
        lax.all_to_all(trial_doubles, VIRT, split_axis=2, concat_axis=1, tiled=True),
        preferred_element_type=jnp.float32,
    ).astype(jnp.bfloat16)
    vv_term = lax.all_to_all(product, VIRT, split_axis=1, concat_axis=2, tiled=True)
    vv_value = vv_term.astype(jnp.float32)
    outer_own = lax.all_to_all(
        outer_part.astype(jnp.bfloat16), "root", split_axis=0, concat_axis=2, tiled=True
    ).astype(outer_part.dtype)
    outer_half = sum_at_owner(outer_own.astype(jnp.bfloat16), "occ", 2)
    summed = vv_value + outer_half - first_term - second_term
    sigma_doubles = (own_active[:, None, None] * summed).astype(jnp.bfloat16)
    trial_piece, sigma_piece = in_one_piece((trial_doubles, sigma_doubles), "root", 2, 0, 1)
    doubles_part = by_axis(flat_pairs(trial_piece, sigma_piece), ROOT_VIRT_OCC)
    singles_part = jnp.dot(
        singles_all.astype(jnp.float32), singles_every.T, precision=lax.Precision.HIGHEST
    )
    whole_matrix = doubles_part / math.sqrt(
        occ_count * occ_count * virt_count
    ) + singles_part / math.sqrt(occ_count)
    subspace = lax.dynamic_slice_in_dim(whole_matrix, root_index * local_roots, local_roots, 0)
    return (sigma_doubles, sigma_singles, subspace)


def solution(mesh):
    torus = Mesh(
        mesh.devices.reshape(mesh.shape["root"], 4, 4, mesh.shape["occ"]),
        ("root", "virt_0", "virt_1", "occ"),
    )
    return jax.shard_map(
        local,
        mesh=torus,
        in_specs=(
            P("root", None),
            P("root", VIRT, "occ"),
            P(),
            P(),
            P("occ", VIRT, "root"),
            P("occ", VIRT, "root"),
            P(),
        ),
        out_specs=(P("root", VIRT, "occ"), P("root", None), P("root", None)),
        check_vma=False,
    )
```

profile of v0, /device:TPU:1, one launch (start us, length us, event | category | flops | bytes accessed | tf_op | source)
XLA Modules:
  0.0 282.3 jit_solution(16731073412498609034)
XLA Ops:
  0.6 5.3 %copy.72 = bf16[2,30,4608]{1,0,2:T(2,128)(2,1)S(1)} copy(bf16[2,30,4608]{2,0,1:T(2,128)(2,1)} %param.8) | data formatting | bytes 1105920 | tf_op args[1]
  5.9 4.5 %reshape.61 = bf16[16,2,8640]{2,1,0:T(2,128)(2,1)S(1)} reshape(bf16[4608,2,30]{2,1,0:T(2,128)(2,1)S(1)} %bitcast.77) | data formatting | bytes 1105920
  10.5 18.6 %all_to_all.90 = bf16[16,2,8640]{2,1,0:T(2,128)(2,1)S(1)} all-to-all(bf16[16,2,8640]{2,1,0:T(2,128)(2,1)S(1)} %reshape.61), channel_id=1, replica_groups=mesh['root'=8,'virt_0'=4,'virt_1'=4,'occ'=2] {'virt_0','virt_1'}, dimensions={0} | all-to-all | bytes 1105920 | tf_op jit(solution)/shard_map/all_to_all | solution.py:109
  29.0 1.6 broadcast_in_dim.12
  30.6 5.5 %all-to-all-start.5 = ((bf16[2,2,30,4608]{3,1,2,0:T(2,128)(2,1)}), bf16[2,2,30,4608]{3,1,2,0:T(2,128)(2,1)S(1)}, u32[]{:S(2)}, u32[]{:S(2)}) async-start(bf16[2,2,30,4608]{3,1,2,0:T(2,128)(2,1)} %broadcast_in_dim.12), calls=%async_computation.5 | async-start | bytes 2211840 | tf_op jit(solution)/shard_map/all_to_all | solution.py:21
  36.1 7.4 %reshape.62 = bf16[4608,2,30]{2,1,0:T(2,128)(2,1)} reshape(bf16[16,2,8640]{2,1,0:T(2,128)(2,1)S(1)} %all_to_all.90) | data formatting | bytes 1105920
  43.5 5.5 %copy.73 = bf16[2,30,16,288]{3,0,1,2:T(2,128)(2,1)S(1)} copy(bf16[2,30,16,288]{1,0,3,2:T(2,128)(2,1)} %bitcast.74) | data formatting | bytes 1105920 | tf_op jit(solution)/shard_map/all_to_all | solution.py:109
  49.6 8.2 %all-to-all-start.2 = ((bf16[8,2,96]{2,1,0:T(2,128)(2,1)}), bf16[8,2,96]{2,1,0:T(2,128)(2,1)S(1)}, u32[]{:S(2)}, u32[]{:S(2)}) async-start(bf16[8,2,96]{2,1,0:T(2,128)(2,1)} %broadcast_in_dim.11), calls=%async_computation.2 | async-start | bytes 8192 | tf_op jit(solution)/shard_map/all_to_all | solution.py:21
  58.4 1.9 copy.75
  60.3 3.9 %all-to-all-done.2 = bf16[8,2,96]{2,1,0:T(2,128)(2,1)S(1)} async-done(((bf16[8,2,96]{2,1,0:T(2,128)(2,1)}), bf16[8,2,96]{2,1,0:T(2,128)(2,1)S(1)}, u32[]{:S(2)}, u32[]{:S(2)}) %all-to-all-start.2) | async-done | bytes 3104 | tf_op jit(solution)/shard_map/all_to_all | solution.py:21
  64.2 4.3 %all-to-all-start.1 = ((bf16[2,480,288]{2,0,1:T(2,128)(2,1)}), bf16[2,480,288]{2,0,1:T(2,128)(2,1)}, u32[]{:S(2)}, u32[]{:S(2)}) async-start(bf16[2,480,288]{2,0,1:T(2,128)(2,1)} %copy.75), calls=%async_computation.1 | async-start | bytes 1474560 | tf_op jit(solution)/shard_map/all_to_all | solution.py:112
  68.5 3.9 %copy.108 = bf16[30,6,8,1152]{3,2,0,1:T(8,128)(2,1)} copy(bf16[30,6,8,1152]{3,2,1,0:T(8,128)(2,1)} %bitcast.83) | data formatting | bytes 6635520 | tf_op jit(solution)/shard_map/reshape | solution.py:104
  72.5 2.7 fusion
  75.1 1.6 convert_element_type.44
  76.7 4.2 %all-to-all-done.1 = bf16[2,480,288]{2,0,1:T(2,128)(2,1)} async-done(((bf16[2,480,288]{2,0,1:T(2,128)(2,1)}), bf16[2,480,288]{2,0,1:T(2,128)(2,1)}, u32[]{:S(2)}, u32[]{:S(2)}) %all-to-all-start.1) | async-done | bytes 552992 | tf_op jit(solution)/shard_map/all_to_all | solution.py:112
  81.0 4.4 %all-to-all-start.3 = ((bf16[16,30,1152]{2,1,0:T(8,128)(2,1)}), bf16[16,30,1152]{2,1,0:T(8,128)(2,1)}, u32[]{:S(2)}, u32[]{:S(2)}) async-start(bf16[16,30,1152]{2,1,0:T(8,128)(2,1)} %convert_element_type.44), calls=%async_computation.3 | async-start | bytes 2359296 | tf_op jit(solution)/shard_map/all_to_all | solution.py:114
  85.4 0.9 copy.84
  86.3 0.9 copy.83
  87.2 8.6 %copy.100 = bf16[2,30,2,4608]{1,0,3,2:T(2,128)(2,1)} copy(bf16[2,30,2,4608]{3,0,1,2:T(2,128)(2,1)S(1)} %bitcast.73) | data formatting | bytes 2211840 | tf_op jit(solution)/shard_map/reshape | solution.py:16
  95.8 1.6 reshape_reshape.3
  97.9 1.8 reshape.48
  100.7 1.8 reshape.50
  102.6 10.4 %reshape.63 = bf16[8,2,34560]{2,1,0:T(2,128)(2,1)} reshape(bf16[9216,2,30]{2,1,0:T(2,128)(2,1)} %bitcast.68) | data formatting | bytes 2211840
  113.1 1.6 convert_bitcast_fusion
  114.8 1.8 reshape.60
  116.6 1.9 copy.123
  118.9 0.9 copy.79
  119.8 7.4 %all_to_all.91 = bf16[2,2,30,4608]{3,1,2,0:T(2,128)(2,1)} all-to-all(bf16[2,2,30,4608]{3,1,2,0:T(2,128)(2,1)S(1)} %copy.79), channel_id=1, replica_groups=mesh['root'=8,'virt_0'=4,'virt_1'=4,'occ'=2] {'occ'}, dimensions={0} | all-to-all | bytes 2211840 | tf_op jit(solution)/shard_map/all_to_all | solution.py:39
  127.2 6.8 %all-to-all-start.6 = ((bf16[8,2,34560]{2,1,0:T(2,128)(2,1)}), bf16[8,2,34560]{2,1,0:T(2,128)(2,1)}, u32[]{:S(2)}, u32[]{:S(2)}) async-start(bf16[8,2,34560]{2,1,0:T(2,128)(2,1)} %reshape.63), calls=%async_computation.6 | async-start | bytes 2211840 | tf_op jit(solution)/shard_map/all_to_all | solution.py:93
  133.9 3.1 %convert_reduce_fusion = f32[2,30,4608]{2,0,1:T(2,128)S(1)} fusion(bf16[2,2,30,4608]{3,1,2,0:T(2,128)(2,1)} %all_to_all.91), kind=kLoop, calls=%fused_computation.2 | loop fusion | flops 829440 | bytes 2211840 | tf_op jit(solution)/shard_map/reduce_sum | solution.py:40
  138.1 1.3 pad_maximum_fusion
  139.4 5.5 %copy.93 = bf16[2,60,4608]{1,0,2:T(2,128)(2,1)S(1)} copy(bf16[2,60,4608]{2,1,0:T(8,128)(2,1)} %pad_maximum_fusion) | data formatting | bytes 2211840 | tf_op jit(solution)/shard_map/concatenate | solution.py:48
  144.9 6.5 %reshape.65 = bf16[8,2,34560]{2,1,0:T(2,128)(2,1)} reshape(bf16[4608,2,60]{2,1,0:T(2,128)(2,1)S(1)} %bitcast.75) | data formatting | bytes 2211840
  151.4 13.1 %all-to-all-done.6 = bf16[8,2,34560]{2,1,0:T(2,128)(2,1)} async-done(((bf16[8,2,34560]{2,1,0:T(2,128)(2,1)}), bf16[8,2,34560]{2,1,0:T(2,128)(2,1)}, u32[]{:S(2)}, u32[]{:S(2)}) %all-to-all-start.6) | async-done | bytes 1105952 | tf_op jit(solution)/shard_map/all_to_all | solution.py:93
  164.5 4.3 %all-to-all-start.7 = ((bf16[8,2,34560]{2,1,0:T(2,128)(2,1)}), bf16[8,2,34560]{2,1,0:T(2,128)(2,1)}, u32[]{:S(2)}, u32[]{:S(2)}) async-start(bf16[8,2,34560]{2,1,0:T(2,128)(2,1)} %reshape.65), calls=%async_computation.7 | async-start | bytes 2211840 | tf_op jit(solution)/shard_map/all_to_all | solution.py:51
  168.8 3.9 %copy.109 = bf16[30,6,8,1152]{3,2,0,1:T(8,128)(2,1)} copy(bf16[30,6,8,1152]{3,2,1,0:T(8,128)(2,1)} %bitcast.84) | data formatting | bytes 6635520 | tf_op jit(solution)/shard_map/reshape | solution.py:61
  172.7 14.0 %reshape.64 = bf16[9216,2,30]{2,1,0:T(2,128)(2,1)} reshape(bf16[8,2,34560]{2,1,0:T(2,128)(2,1)} %all-to-all-done.6) | data formatting | bytes 2211840
  186.7 10.4 %copy.102 = bf16[2,30,8,1152]{3,1,0,2:T(8,128)(2,1)S(1)} copy(bf16[2,30,8,1152]{1,0,3,2:T(2,128)(2,1)} %bitcast.69) | data formatting | bytes 2211840 | tf_op jit(solution)/shard_map/all_to_all | solution.py:93
  197.4 2.9 %fusion.21 = f32[16,48]{1,0:T(8,128)S(1)} fusion(bf16[16,34560]{1,0:T(8,128)(2,1)S(1)} %bitcast.80, bf16[48,34560]{1,0:T(8,128)(2,1)} %bitcast.70), kind=kOutput, calls=%fused_computation.36 | convolution fusion | flops 53084160 | bytes 4426752 | tf_op jit(solution)/shard_map/dot_general | solution.py:59
  200.6 1.4 copy.96
  201.9 8.2 %reshape.66 = bf16[4608,2,60]{2,1,0:T(2,128)(2,1)S(1)} reshape(bf16[8,2,34560]{2,1,0:T(2,128)(2,1)} %all-to-all-done.7) | data formatting | bytes 2211840
  210.1 3.4 %copy.103 = bf16[2,60,8,576]{3,2,0,1:T(8,128)(2,1)} copy(bf16[2,60,8,576]{1,0,3,2:T(2,128)(2,1)S(1)} %bitcast.76) | data formatting | bytes 2211840 | tf_op jit(solution)/shard_map/all_to_all | solution.py:51
  213.6 2.3 copy.95
  215.8 1.0 all_to_all.81
  217.2 22.8 %all-reduce = (f32[16,96]{1,0:T(8,128)S(1)}, f32[16,16]{1,0:T(8,128)S(1)}) all-reduce(f32[16,96]{1,0:T(8,128)S(1)} %dynamic_update_slice.3, f32[16,16]{1,0:T(8,128)S(1)} %convolution_bitcast_fusion.1), channel_id=1, replica_groups=mesh['root'=8,'virt_0'=4,'virt_1'=4,'occ'=2] {'root'}, use_global_device_ids=true, to_apply=%region_1.0 | all-reduce | flops 1792 | bytes 14336 | tf_op jit(solution)/shard_map/psum | solution.py:29
  240.1 11.4 %all-reduce.2 = (f32[16,96]{1,0:T(8,128)S(1)}, f32[16,16]{1,0:T(8,128)S(1)}) all-reduce(f32[16,96]{1,0:T(8,128)S(1)} %get-tuple-element.12, f32[16,16]{1,0:T(8,128)S(1)} %get-tuple-element.13), channel_id=1, replica_groups=mesh['root'=8,'virt_0'=4,'virt_1'=4,'occ'=2] {'virt_0'}, use_global_device_ids=true, to_apply=%region_2.0 | all-reduce | flops 1792 | bytes 14336 | tf_op jit(solution)/shard_map/psum | solution.py:29
  251.4 11.2 %all-reduce.1 = (f32[16,96]{1,0:T(8,128)S(1)}, f32[16,16]{1,0:T(8,128)S(1)}) all-reduce(f32[16,96]{1,0:T(8,128)S(1)} %get-tuple-element.16, f32[16,16]{1,0:T(8,128)S(1)} %get-tuple-element.17), channel_id=1, replica_groups=mesh['root'=8,'virt_0'=4,'virt_1'=4,'occ'=2] {'virt_1'}, use_global_device_ids=true, to_apply=%region_3.0 | all-reduce | flops 1792 | bytes 14336 | tf_op jit(solution)/shard_map/psum | solution.py:29
  262.6 18.3 %all-reduce.3 = (f32[16,96]{1,0:T(8,128)S(1)}, f32[16,16]{1,0:T(8,128)S(1)}) all-reduce(f32[16,96]{1,0:T(8,128)S(1)} %get-tuple-element.14, f32[16,16]{1,0:T(8,128)S(1)} %get-tuple-element.15), channel_id=1, replica_groups=mesh['root'=8,'virt_0'=4,'virt_1'=4,'occ'=2] {'occ'}, use_global_device_ids=true, to_apply=%region_4.0 | all-reduce | flops 1792 | bytes 14336 | tf_op jit(solution)/shard_map/psum | solution.py:29
  (43 shorter events, 6.9 us)
Async XLA Ops:
  0.6 57.1 %copy-start = (bf16[480,480]{1,0:T(8,128)(2,1)S(1)}, bf16[480,480]{1,0:T(8,128)(2,1)}, u32[]{:S(2)}) copy-start(bf16[480,480]{1,0:T(8,128)(2,1)} %param.10) | copy-start | bytes 1382404
  10.5 18.6 %copy-start.4 = (bf16[2,30,4608]{2,0,1:T(2,128)(2,1)S(1)}, bf16[2,30,4608]{2,0,1:T(2,128)(2,1)}, u32[]{:S(2)}) copy-start(bf16[2,30,4608]{2,0,1:T(2,128)(2,1)} %param.8) | copy-start | bytes 1658884
  30.6 18.4 %all-to-all-start.5 = ((bf16[2,2,30,4608]{3,1,2,0:T(2,128)(2,1)}), bf16[2,2,30,4608]{3,1,2,0:T(2,128)(2,1)S(1)}, u32[]{:S(2)}, u32[]{:S(2)}) async-start(bf16[2,2,30,4608]{3,1,2,0:T(2,128)(2,1)} %broadcast_in_dim.12), calls=%async_computation.5 | async-start | bytes 2211840 | tf_op jit(solution)/shard_map/all_to_all | solution.py:21
  43.5 5.5 %copy-start.9 = (bf16[2,96]{1,0:T(2,128)(2,1)S(1)}, bf16[2,96]{1,0:T(2,128)(2,1)}, u32[]{:S(2)}) copy-start(bf16[2,96]{1,0:T(2,128)(2,1)} %param.7) | copy-start | bytes 1156
  49.6 14.7 %all-to-all-start.2 = ((bf16[8,2,96]{2,1,0:T(2,128)(2,1)}), bf16[8,2,96]{2,1,0:T(2,128)(2,1)S(1)}, u32[]{:S(2)}, u32[]{:S(2)}) async-start(bf16[8,2,96]{2,1,0:T(2,128)(2,1)} %broadcast_in_dim.11), calls=%async_computation.2 | async-start | bytes 8192 | tf_op jit(solution)/shard_map/all_to_all | solution.py:21
  64.2 16.7 %all-to-all-start.1 = ((bf16[2,480,288]{2,0,1:T(2,128)(2,1)}), bf16[2,480,288]{2,0,1:T(2,128)(2,1)}, u32[]{:S(2)}, u32[]{:S(2)}) async-start(bf16[2,480,288]{2,0,1:T(2,128)(2,1)} %copy.75), calls=%async_computation.1 | async-start | bytes 1474560 | tf_op jit(solution)/shard_map/all_to_all | solution.py:112
  81.0 35.6 %all-to-all-start.3 = ((bf16[16,30,1152]{2,1,0:T(8,128)(2,1)}), bf16[16,30,1152]{2,1,0:T(8,128)(2,1)}, u32[]{:S(2)}, u32[]{:S(2)}) async-start(bf16[16,30,1152]{2,1,0:T(8,128)(2,1)} %convert_element_type.44), calls=%async_computation.3 | async-start | bytes 2359296 | tf_op jit(solution)/shard_map/all_to_all | solution.py:114
  95.8 1.6 copy-start.8
  97.9 1.8 copy-start.2
  102.6 10.4 %copy-start.10 = (s32[16]{0:T(128)S(1)}, s32[16]{0:T(128)}, u32[]{:S(2)}) copy-start(s32[16]{0:T(128)} %param.13) | copy-start | bytes 196
  127.2 9.9 %copy-start.6 = (f32[2,30,4608]{2,1,0:T(8,128)S(1)}, f32[2,30,4608]{2,1,0:T(8,128)}, u32[]{:S(2)}) copy-start(f32[2,30,4608]{2,1,0:T(8,128)} %reshape.50) | copy-start | bytes 3317764
  127.2 9.9 %copy-start.7 = (f32[2,30,4608]{2,1,0:T(8,128)S(1)}, f32[2,30,4608]{2,1,0:T(8,128)}, u32[]{:S(2)}) copy-start(f32[2,30,4608]{2,1,0:T(8,128)} %reshape.60) | copy-start | bytes 3317764
  127.2 37.3 %all-to-all-start.6 = ((bf16[8,2,34560]{2,1,0:T(2,128)(2,1)}), bf16[8,2,34560]{2,1,0:T(2,128)(2,1)}, u32[]{:S(2)}, u32[]{:S(2)}) async-start(bf16[8,2,34560]{2,1,0:T(2,128)(2,1)} %reshape.63), calls=%async_computation.6 | async-start | bytes 2211840 | tf_op jit(solution)/shard_map/all_to_all | solution.py:93
  133.9 3.1 %copy-start.5 = (f32[2,30,4608]{2,1,0:T(8,128)S(1)}, f32[2,30,4608]{2,1,0:T(8,128)}, u32[]{:S(2)}) copy-start(f32[2,30,4608]{2,1,0:T(8,128)} %reshape.48) | copy-start | bytes 3317764
  137.1 1.1 copy-start.3
  164.5 37.4 %all-to-all-start.7 = ((bf16[8,2,34560]{2,1,0:T(2,128)(2,1)}), bf16[8,2,34560]{2,1,0:T(2,128)(2,1)}, u32[]{:S(2)}, u32[]{:S(2)}) async-start(bf16[8,2,34560]{2,1,0:T(2,128)(2,1)} %reshape.65), calls=%async_computation.7 | async-start | bytes 2211840 | tf_op jit(solution)/shard_map/all_to_all | solution.py:51
  215.8 66.5 %copy-start.1 = (bf16[480,480]{1,0:T(8,128)(2,1)S(1)}, bf16[480,480]{1,0:T(8,128)(2,1)}, u32[]{:S(2)}) copy-start(bf16[480,480]{1,0:T(8,128)(2,1)} %param.10) | copy-start | bytes 1382404
where the time goes:
time: 284 us; the launch traced here: 282 us
  local copies, waits for them, and re-layouts  122 us (43%)
  blocking collectives  89.6 us (32%)
  starting transfers between devices  33.4 us (12%)
  waiting for transfers between devices  21.3 us (8%)
  matrix products  7.62 us (3%)
  other arithmetic  7.03 us (2%)
    psum x4, blocking collectives, by_axis(): return functools.reduce(lax.psum, axes, array)  63.7 us
    unnamed x32, local copies, waits for them, and re-layouts  59.5 us
    all_to_all x1, blocking collectives, local(): lax.all_to_all(trial_doubles, VIRT, split_axis=2, concat_axis=1, tiled=True)  18.6 us
    all_to_all x2, starting transfers between devices, from_everyone(): return lax.all_to_all(copies, axis, split_axis=0, concat_axis=0, tiled=True)  13.7 us
    all_to_all x1, waiting for transfers between devices, local(): lax.all_to_all(gathered, 'root', split_axis=2, concat_axis=0, tiled=True)  13.1 us
    all_to_all x1, local copies, waits for them, and re-layouts, local(): lax.all_to_all(gathered, 'root', split_axis=2, concat_axis=0, tiled=True)  10.4 us
    reshape x1, local copies, waits for them, and re-layouts, laid_out(): parts.reshape(*shape[:dim], shape[dim] * shape[dim + 1], *shape[dim + 2:])  8.62 us
    all_to_all x1, blocking collectives, sum_at_owner(): lax.all_to_all(parts, axis, split_axis=0, concat_axis=0, tiled=True)  7.36 us
  transfers between devices with their start and end apart: 6, of which 3 were waited for; matrix products, arithmetic and copies ran while one was open for 37% of the time, Pallas kernels for 0%

commit v1 on v0

--- a/solution.py
+++ b/solution.py
@@ -106,7 +106,12 @@
     product = jnp.einsum(
         "ac,ncp->nap",
         virt_fock,
-        lax.all_to_all(trial_doubles, VIRT, split_axis=2, concat_axis=1, tiled=True),
+        jnp.concatenate(
+            lax.all_to_all(
+                jnp.stack(jnp.split(trial_doubles, lax.axis_size(VIRT), axis=2)), VIRT, 0, 0
+            ),
+            axis=1,
+        ),
         preferred_element_type=jnp.float32,
     ).astype(jnp.bfloat16)
     vv_term = lax.all_to_all(product, VIRT, split_axis=1, concat_axis=2, tiled=True)

time: 284 us -> 265 us (0.933)
  local copies, waits for them, and re-layouts: 122 us -> 103 us
    unnamed x32 -> x44, local copies, waits for them, and re-layouts: 59.5 us -> 44 us
    all_to_all x1 -> x0, local copies, waits for them, and re-layouts: 5.49 us -> none  [local(): lax.all_to_all(trial_doubles, VIRT, split_axis=2, concat_axis=1, tiled=True)]
  transfers between devices with their start and end apart: 6 -> 6, of which waited for: 3 -> 3; matrix products, arithmetic and copies ran while one was open for 37% -> 36% of each run, Pallas kernels for 0% -> 0%
where the time goes in v1:
time: 265 us; the launch traced here: 264 us
  local copies, waits for them, and re-layouts  103 us (39%)
  blocking collectives  91 us (34%)
  starting transfers between devices  34.9 us (13%)
  waiting for transfers between devices  18.6 us (7%)
  matrix products  8.63 us (3%)
  other arithmetic  7.03 us (3%)
    psum x4, blocking collectives, by_axis(): return functools.reduce(lax.psum, axes, array)  64.2 us
    unnamed x44, local copies, waits for them, and re-layouts  44 us
    all_to_all x1, blocking collectives, local(): lax.all_to_all(jnp.stack(jnp.split(trial_doubles, lax.axis_size(VIRT), ax...  17.7 us
    all_to_all x2, starting transfers between devices, from_everyone(): return lax.all_to_all(copies, axis, split_axis=0, concat_axis=0, tiled=True)  15.1 us
    all_to_all x1, waiting for transfers between devices, local(): lax.all_to_all(gathered, 'root', split_axis=2, concat_axis=0, tiled=True)  13.1 us
    all_to_all x1, local copies, waits for them, and re-layouts, local(): lax.all_to_all(gathered, 'root', split_axis=2, concat_axis=0, tiled=True)  10.4 us
    all_to_all x1, blocking collectives, sum_at_owner(): lax.all_to_all(parts, axis, split_axis=0, concat_axis=0, tiled=True)  9.03 us
    reshape x1, local copies, waits for them, and re-layouts, laid_out(): parts.reshape(*shape[:dim], shape[dim] * shape[dim + 1], *shape[dim + 2:])  8.62 us
  transfers between devices with their start and end apart: 6, of which 3 were waited for; matrix products, arithmetic and copies ran while one was open for 36% of the time, Pallas kernels for 0%

profile of v1, /device:TPU:1, one launch (start us, length us, event | category | flops | bytes accessed | tf_op | source)
XLA Modules:
  0.0 263.7 jit_solution(7737383282119343814)
XLA Ops:
  0.6 2.7 %broadcast_in_dim.12 = bf16[2,2,30,4608]{3,1,2,0:T(2,128)(2,1)} broadcast(bf16[2,30,4608]{2,0,1:T(2,128)(2,1)} %param.8), dimensions={1,2,3} | broadcast | bytes 1658880 | tf_op jit(solution)/shard_map/broadcast_in_dim | solution.py:20
  3.3 6.9 %all-to-all-start.5 = ((bf16[2,2,30,4608]{3,1,2,0:T(2,128)(2,1)}), bf16[2,2,30,4608]{3,1,2,0:T(2,128)(2,1)S(1)}, u32[]{:S(2)}, u32[]{:S(2)}) async-start(bf16[2,2,30,4608]{3,1,2,0:T(2,128)(2,1)} %broadcast_in_dim.12), calls=%async_computation.5 | async-start | bytes 2211840 | tf_op jit(solution)/shard_map/all_to_all | solution.py:21
  12.1 17.7 %all_to_all.77 = bf16[16,2,30,288]{3,1,2,0:T(2,128)(2,1)} all-to-all(bf16[16,2,30,288]{3,1,2,0:T(2,128)(2,1)S(1)} %bitcast_dynamic-update-slice_fusion), channel_id=1, replica_groups=mesh['root'=8,'virt_0'=4,'virt_1'=4,'occ'=2] {'virt_0','virt_1'}, dimensions={0} | all-to-all | bytes 1105920 | tf_op jit(solution)/shard_map/all_to_all | solution.py:110
  29.8 0.6 broadcast_in_dim.11
  30.4 8.2 %all-to-all-start.2 = ((bf16[8,2,96]{2,1,0:T(2,128)(2,1)}), bf16[8,2,96]{2,1,0:T(2,128)(2,1)S(1)}, u32[]{:S(2)}, u32[]{:S(2)}) async-start(bf16[8,2,96]{2,1,0:T(2,128)(2,1)} %broadcast_in_dim.11), calls=%async_computation.2 | async-start | bytes 8192 | tf_op jit(solution)/shard_map/all_to_all | solution.py:21
  38.6 1.8 fusion.1
  40.3 1.9 copy.69
  42.2 2.8 %all-to-all-done.2 = bf16[8,2,96]{2,1,0:T(2,128)(2,1)S(1)} async-done(((bf16[8,2,96]{2,1,0:T(2,128)(2,1)}), bf16[8,2,96]{2,1,0:T(2,128)(2,1)S(1)}, u32[]{:S(2)}, u32[]{:S(2)}) %all-to-all-start.2) | async-done | bytes 3104 | tf_op jit(solution)/shard_map/all_to_all | solution.py:21
  45.0 4.3 %all-to-all-start.1 = ((bf16[2,480,288]{2,0,1:T(2,128)(2,1)}), bf16[2,480,288]{2,0,1:T(2,128)(2,1)}, u32[]{:S(2)}, u32[]{:S(2)}) async-start(bf16[2,480,288]{2,0,1:T(2,128)(2,1)} %copy.69), calls=%async_computation.1 | async-start | bytes 1474560 | tf_op jit(solution)/shard_map/all_to_all | solution.py:117
  49.3 3.9 %copy.102 = bf16[30,6,8,1152]{3,2,0,1:T(8,128)(2,1)} copy(bf16[30,6,8,1152]{3,2,1,0:T(8,128)(2,1)} %bitcast.110) | data formatting | bytes 6635520 | tf_op jit(solution)/shard_map/reshape | solution.py:104
  53.2 2.6 fusion
  55.8 1.6 convert_element_type.44
  57.4 2.7 %all-to-all-done.1 = bf16[2,480,288]{2,0,1:T(2,128)(2,1)} async-done(((bf16[2,480,288]{2,0,1:T(2,128)(2,1)}), bf16[2,480,288]{2,0,1:T(2,128)(2,1)}, u32[]{:S(2)}, u32[]{:S(2)}) %all-to-all-start.1) | async-done | bytes 552992 | tf_op jit(solution)/shard_map/all_to_all | solution.py:117
  60.1 4.4 %all-to-all-start.3 = ((bf16[16,30,1152]{2,1,0:T(8,128)(2,1)}), bf16[16,30,1152]{2,1,0:T(8,128)(2,1)}, u32[]{:S(2)}, u32[]{:S(2)}) async-start(bf16[16,30,1152]{2,1,0:T(8,128)(2,1)} %convert_element_type.44), calls=%async_computation.3 | async-start | bytes 2359296 | tf_op jit(solution)/shard_map/all_to_all | solution.py:119
  64.5 0.9 copy.78
  65.4 0.9 copy.77
  66.3 8.6 %copy.94 = bf16[2,30,2,4608]{1,0,3,2:T(2,128)(2,1)} copy(bf16[2,30,2,4608]{3,0,1,2:T(2,128)(2,1)S(1)} %bitcast.102) | data formatting | bytes 2211840 | tf_op jit(solution)/shard_map/reshape | solution.py:16
  74.9 1.6 reshape_reshape.3
  77.0 1.8 reshape.56
  78.8 0.7 reshape.57
  79.8 1.8 reshape.58
  81.7 10.4 %reshape.69 = bf16[8,2,34560]{2,1,0:T(2,128)(2,1)} reshape(bf16[9216,2,30]{2,1,0:T(2,128)(2,1)} %bitcast.97) | data formatting | bytes 2211840
  92.2 1.6 convert_bitcast_fusion
  93.9 1.8 reshape.68
  95.7 1.9 copy.117
  98.0 0.9 copy.73
  98.9 9.0 %all_to_all.78 = bf16[2,2,30,4608]{3,1,2,0:T(2,128)(2,1)} all-to-all(bf16[2,2,30,4608]{3,1,2,0:T(2,128)(2,1)S(1)} %copy.73), channel_id=1, replica_groups=mesh['root'=8,'virt_0'=4,'virt_1'=4,'occ'=2] {'occ'}, dimensions={0} | all-to-all | bytes 2211840 | tf_op jit(solution)/shard_map/all_to_all | solution.py:39
  108.0 6.8 %all-to-all-start.6 = ((bf16[8,2,34560]{2,1,0:T(2,128)(2,1)}), bf16[8,2,34560]{2,1,0:T(2,128)(2,1)}, u32[]{:S(2)}, u32[]{:S(2)}) async-start(bf16[8,2,34560]{2,1,0:T(2,128)(2,1)} %reshape.69), calls=%async_computation.6 | async-start | bytes 2211840 | tf_op jit(solution)/shard_map/all_to_all | solution.py:93
  114.7 3.1 %convert_reduce_fusion = f32[2,30,4608]{2,0,1:T(2,128)S(1)} fusion(bf16[2,2,30,4608]{3,1,2,0:T(2,128)(2,1)} %all_to_all.78), kind=kLoop, calls=%fused_computation.2 | loop fusion | flops 829440 | bytes 2211840 | tf_op jit(solution)/shard_map/reduce_sum | solution.py:40
  118.9 1.3 pad_maximum_fusion
  120.2 5.5 %copy.87 = bf16[2,60,4608]{1,0,2:T(2,128)(2,1)S(1)} copy(bf16[2,60,4608]{2,1,0:T(8,128)(2,1)} %pad_maximum_fusion) | data formatting | bytes 2211840 | tf_op jit(solution)/shard_map/concatenate | solution.py:48
  125.7 6.5 %reshape.71 = bf16[8,2,34560]{2,1,0:T(2,128)(2,1)} reshape(bf16[4608,2,60]{2,1,0:T(2,128)(2,1)S(1)} %bitcast.103) | data formatting | bytes 2211840
  132.2 13.1 %all-to-all-done.6 = bf16[8,2,34560]{2,1,0:T(2,128)(2,1)} async-done(((bf16[8,2,34560]{2,1,0:T(2,128)(2,1)}), bf16[8,2,34560]{2,1,0:T(2,128)(2,1)}, u32[]{:S(2)}, u32[]{:S(2)}) %all-to-all-start.6) | async-done | bytes 1105952 | tf_op jit(solution)/shard_map/all_to_all | solution.py:93
  145.3 4.3 %all-to-all-start.7 = ((bf16[8,2,34560]{2,1,0:T(2,128)(2,1)}), bf16[8,2,34560]{2,1,0:T(2,128)(2,1)}, u32[]{:S(2)}, u32[]{:S(2)}) async-start(bf16[8,2,34560]{2,1,0:T(2,128)(2,1)} %reshape.71), calls=%async_computation.7 | async-start | bytes 2211840 | tf_op jit(solution)/shard_map/all_to_all | solution.py:51
  149.6 3.9 %copy.103 = bf16[30,6,8,1152]{3,2,0,1:T(8,128)(2,1)} copy(bf16[30,6,8,1152]{3,2,1,0:T(8,128)(2,1)} %bitcast.111) | data formatting | bytes 6635520 | tf_op jit(solution)/shard_map/reshape | solution.py:61
  153.5 14.0 %reshape.70 = bf16[9216,2,30]{2,1,0:T(2,128)(2,1)} reshape(bf16[8,2,34560]{2,1,0:T(2,128)(2,1)} %all-to-all-done.6) | data formatting | bytes 2211840
  167.4 10.4 %copy.96 = bf16[2,30,8,1152]{3,1,0,2:T(8,128)(2,1)S(1)} copy(bf16[2,30,8,1152]{1,0,3,2:T(2,128)(2,1)} %bitcast.98) | data formatting | bytes 2211840 | tf_op jit(solution)/shard_map/all_to_all | solution.py:93
  178.2 2.9 %fusion.21 = f32[16,48]{1,0:T(8,128)S(1)} fusion(bf16[16,34560]{1,0:T(8,128)(2,1)S(1)} %bitcast.107, bf16[48,34560]{1,0:T(8,128)(2,1)} %bitcast.99), kind=kOutput, calls=%fused_computation.52 | convolution fusion | flops 53084160 | bytes 4426752 | tf_op jit(solution)/shard_map/dot_general | solution.py:59
  181.4 1.4 copy.90
  182.7 8.2 %reshape.72 = bf16[4608,2,60]{2,1,0:T(2,128)(2,1)S(1)} reshape(bf16[8,2,34560]{2,1,0:T(2,128)(2,1)} %all-to-all-done.7) | data formatting | bytes 2211840
  190.9 3.4 %copy.97 = bf16[2,60,8,576]{3,2,0,1:T(8,128)(2,1)} copy(bf16[2,60,8,576]{1,0,3,2:T(2,128)(2,1)S(1)} %bitcast.104) | data formatting | bytes 2211840 | tf_op jit(solution)/shard_map/all_to_all | solution.py:51
  194.4 2.3 copy.89
  196.6 1.0 all_to_all.68
  198.0 22.8 %all-reduce = (f32[16,96]{1,0:T(8,128)S(1)}, f32[16,16]{1,0:T(8,128)S(1)}) all-reduce(f32[16,96]{1,0:T(8,128)S(1)} %dynamic_update_slice.3, f32[16,16]{1,0:T(8,128)S(1)} %convolution_bitcast_fusion.1), channel_id=1, replica_groups=mesh['root'=8,'virt_0'=4,'virt_1'=4,'occ'=2] {'root'}, use_global_device_ids=true, to_apply=%region_1.0 | all-reduce | flops 1792 | bytes 14336 | tf_op jit(solution)/shard_map/psum | solution.py:29
  220.9 11.3 %all-reduce.2 = (f32[16,96]{1,0:T(8,128)S(1)}, f32[16,16]{1,0:T(8,128)S(1)}) all-reduce(f32[16,96]{1,0:T(8,128)S(1)} %get-tuple-element.12, f32[16,16]{1,0:T(8,128)S(1)} %get-tuple-element.13), channel_id=1, replica_groups=mesh['root'=8,'virt_0'=4,'virt_1'=4,'occ'=2] {'virt_0'}, use_global_device_ids=true, to_apply=%region_2.0 | all-reduce | flops 1792 | bytes 14336 | tf_op jit(solution)/shard_map/psum | solution.py:29
  232.2 11.9 %all-reduce.1 = (f32[16,96]{1,0:T(8,128)S(1)}, f32[16,16]{1,0:T(8,128)S(1)}) all-reduce(f32[16,96]{1,0:T(8,128)S(1)} %get-tuple-element.16, f32[16,16]{1,0:T(8,128)S(1)} %get-tuple-element.17), channel_id=1, replica_groups=mesh['root'=8,'virt_0'=4,'virt_1'=4,'occ'=2] {'virt_1'}, use_global_device_ids=true, to_apply=%region_3.0 | all-reduce | flops 1792 | bytes 14336 | tf_op jit(solution)/shard_map/psum | solution.py:29
  244.2 18.1 %all-reduce.3 = (f32[16,96]{1,0:T(8,128)S(1)}, f32[16,16]{1,0:T(8,128)S(1)}) all-reduce(f32[16,96]{1,0:T(8,128)S(1)} %get-tuple-element.14, f32[16,16]{1,0:T(8,128)S(1)} %get-tuple-element.15), channel_id=1, replica_groups=mesh['root'=8,'virt_0'=4,'virt_1'=4,'occ'=2] {'occ'}, use_global_device_ids=true, to_apply=%region_4.0 | all-reduce | flops 1792 | bytes 14336 | tf_op jit(solution)/shard_map/psum | solution.py:29
  262.5 0.6 constant_dynamic-slice_fusion.2
  (55 shorter events, 6.1 us)
Async XLA Ops:
  0.6 37.9 %copy-start = (bf16[480,480]{1,0:T(8,128)(2,1)S(1)}, bf16[480,480]{1,0:T(8,128)(2,1)}, u32[]{:S(2)}) copy-start(bf16[480,480]{1,0:T(8,128)(2,1)} %param.10) | copy-start | bytes 1382404
  3.3 6.9 %copy-start.2 = (bf16[2,30,4608]{2,0,1:T(2,128)(2,1)S(1)}, bf16[2,30,4608]{2,0,1:T(2,128)(2,1)}, u32[]{:S(2)}) copy-start(bf16[2,30,4608]{2,0,1:T(2,128)(2,1)} %param.8) | copy-start | bytes 1658884
  3.3 8.7 %all-to-all-start.5 = ((bf16[2,2,30,4608]{3,1,2,0:T(2,128)(2,1)}), bf16[2,2,30,4608]{3,1,2,0:T(2,128)(2,1)S(1)}, u32[]{:S(2)}, u32[]{:S(2)}) async-start(bf16[2,2,30,4608]{3,1,2,0:T(2,128)(2,1)} %broadcast_in_dim.12), calls=%async_computation.5 | async-start | bytes 2211840 | tf_op jit(solution)/shard_map/all_to_all | solution.py:21
  10.9 18.9 %copy-start.9 = (bf16[2,96]{1,0:T(2,128)(2,1)S(1)}, bf16[2,96]{1,0:T(2,128)(2,1)}, u32[]{:S(2)}) copy-start(bf16[2,96]{1,0:T(2,128)(2,1)} %param.7) | copy-start | bytes 1156
  30.4 14.7 %all-to-all-start.2 = ((bf16[8,2,96]{2,1,0:T(2,128)(2,1)}), bf16[8,2,96]{2,1,0:T(2,128)(2,1)S(1)}, u32[]{:S(2)}, u32[]{:S(2)}) async-start(bf16[8,2,96]{2,1,0:T(2,128)(2,1)} %broadcast_in_dim.11), calls=%async_computation.2 | async-start | bytes 8192 | tf_op jit(solution)/shard_map/all_to_all | solution.py:21
  45.0 15.0 %all-to-all-start.1 = ((bf16[2,480,288]{2,0,1:T(2,128)(2,1)}), bf16[2,480,288]{2,0,1:T(2,128)(2,1)}, u32[]{:S(2)}, u32[]{:S(2)}) async-start(bf16[2,480,288]{2,0,1:T(2,128)(2,1)} %copy.69), calls=%async_computation.1 | async-start | bytes 1474560 | tf_op jit(solution)/shard_map/all_to_all | solution.py:117
  60.1 35.6 %all-to-all-start.3 = ((bf16[16,30,1152]{2,1,0:T(8,128)(2,1)}), bf16[16,30,1152]{2,1,0:T(8,128)(2,1)}, u32[]{:S(2)}, u32[]{:S(2)}) async-start(bf16[16,30,1152]{2,1,0:T(8,128)(2,1)} %convert_element_type.44), calls=%async_computation.3 | async-start | bytes 2359296 | tf_op jit(solution)/shard_map/all_to_all | solution.py:119
  74.9 1.6 copy-start.8
  77.0 1.8 copy-start.3
  81.7 10.4 %copy-start.10 = (s32[16]{0:T(128)S(1)}, s32[16]{0:T(128)}, u32[]{:S(2)}) copy-start(s32[16]{0:T(128)} %param.13) | copy-start | bytes 196
  107.9 9.9 %copy-start.6 = (f32[2,30,4608]{2,1,0:T(8,128)S(1)}, f32[2,30,4608]{2,1,0:T(8,128)}, u32[]{:S(2)}) copy-start(f32[2,30,4608]{2,1,0:T(8,128)} %reshape.58) | copy-start | bytes 3317764
  107.9 9.9 %copy-start.7 = (f32[2,30,4608]{2,1,0:T(8,128)S(1)}, f32[2,30,4608]{2,1,0:T(8,128)}, u32[]{:S(2)}) copy-start(f32[2,30,4608]{2,1,0:T(8,128)} %reshape.68) | copy-start | bytes 3317764
  108.0 37.4 %all-to-all-start.6 = ((bf16[8,2,34560]{2,1,0:T(2,128)(2,1)}), bf16[8,2,34560]{2,1,0:T(2,128)(2,1)}, u32[]{:S(2)}, u32[]{:S(2)}) async-start(bf16[8,2,34560]{2,1,0:T(2,128)(2,1)} %reshape.69), calls=%async_computation.6 | async-start | bytes 2211840 | tf_op jit(solution)/shard_map/all_to_all | solution.py:93
  114.7 3.1 %copy-start.5 = (f32[2,30,4608]{2,1,0:T(8,128)S(1)}, f32[2,30,4608]{2,1,0:T(8,128)}, u32[]{:S(2)}) copy-start(f32[2,30,4608]{2,1,0:T(8,128)} %reshape.56) | copy-start | bytes 3317764
  117.9 1.1 copy-start.4
  145.3 37.4 %all-to-all-start.7 = ((bf16[8,2,34560]{2,1,0:T(2,128)(2,1)}), bf16[8,2,34560]{2,1,0:T(2,128)(2,1)}, u32[]{:S(2)}, u32[]{:S(2)}) async-start(bf16[8,2,34560]{2,1,0:T(2,128)(2,1)} %reshape.71), calls=%async_computation.7 | async-start | bytes 2211840 | tf_op jit(solution)/shard_map/all_to_all | solution.py:51
  196.6 67.0 %copy-start.1 = (bf16[480,480]{1,0:T(8,128)(2,1)S(1)}, bf16[480,480]{1,0:T(8,128)(2,1)}, u32[]{:S(2)}) copy-start(bf16[480,480]{1,0:T(8,128)(2,1)} %param.10) | copy-start | bytes 1382404
